TPU v7x, 32 devices: a whole 2x2x4 slice. The times are simulated.
32 devices in a mesh: dp: 4 (over x, core), pipe: 4 (over z), tensor: 2 (over y).
Axes of the slice: x: 2, y: 2, z: 4, core: 2. Of those that a mesh axis runs over, the one named last changes fastest.
Arguments:
- support_tokens: int32 [32, 32], P(('dp', 'pipe')), may hold values from 0 to 64127
- support_lengths: int32 [32], P(('dp', 'pipe')), may hold values from 1 to 32
- support_labels: int32 [32, 1], P(('dp', 'pipe')), may hold values from 0 to 31
- query_tokens: int32 [16, 32], P(('dp', 'pipe')), may hold values from 0 to 64127
- query_lengths: int32 [16], P(('dp', 'pipe')), may hold values from 1 to 32
- query_episodes: int32 [16], P(('dp', 'pipe')), may hold values from 0 to 1
- embedding: bfloat16 [64128, 4096], P(('dp', 'pipe'), 'tensor'), may hold values from -18 to 18
- attn_gain: float32 [4, 4096], P('pipe'), may hold values from 0.5 to 1.5
- query_weight: bfloat16 [4, 4096, 4096], P('pipe', None, 'tensor'), may hold values from -1 to 1
- key_weight: bfloat16 [4, 4096, 1024], P('pipe', None, 'tensor'), may hold values from -16 to 16
- value_weight: bfloat16 [4, 4096, 1024], P('pipe', None, 'tensor'), may hold values from -0.09375 to 0.09375
- out_weight: bfloat16 [4, 4096, 4096], P('pipe', 'tensor'), may hold values from -0.09375 to 0.09375
- final_gain: float32 [4096], replicated, may hold values from 0.5 to 1.5
Outputs:
- prototypes: float32 [32, 4096], P(None, 'tensor')
- logits: float32 [16, 16], P(('dp', 'pipe'))
Inputs may be any that keep to these rules, and one draw needn't show every extreme that they name: `support_labels`: every class is the label of at least one support sequence.
All inputs are finite; a program needn't handle non-finite values.
Results may differ from a plain program's by a relative error of at most 0.024.
Values may be sent and summed in bfloat16 or wider, within the bound.
No kernel may reach another device: no remote copies, remote signals or barrier semaphores. Data moves between devices by JAX's collectives and lax.ppermute only.
A program may use at most 128 MiB of HBM per device.

v0:
```python
import math
import jax
import jax.numpy as jnp
from jax import lax
from jax.sharding import PartitionSpec as P

D = 4096
HEAD_DIM = 128
WAYS = 16
EPISODES = 2
epsilon = 1e-05
rotary_base = 500000.0


def passed_along(block, axis, distance):
    devices = range(lax.axis_size(axis))
    route = [((i - distance) % len(devices), i) for i in devices]
    return lax.ppermute(block, axis, route)


def rotate(heads_in, seq_len):
    half_dim = HEAD_DIM // 2
    freqs = jnp.exp(
        -math.log(rotary_base) * jnp.arange(half_dim, dtype=jnp.float32) * (2.0 / HEAD_DIM)
    )
    angles = jnp.arange(seq_len, dtype=jnp.float32)[:, None] * freqs[None, :]
    cosine = jnp.cos(angles)[None, :, None, :]
    sine = jnp.sin(angles)[None, :, None, :]
    first_half = heads_in[..., :half_dim]
    second_half = heads_in[..., half_dim:]
    return jnp.concatenate(
        [first_half * cosine - second_half * sine, second_half * cosine + first_half * sine],
        axis=-1,
    )


def whole_rows(hidden):
    return lax.all_gather(hidden, "tensor", axis=1, tiled=True)


def whole_values(full_rows, gain_vector):
    values = full_rows.astype(jnp.float32)
    mean_square = jnp.mean(values * values, axis=-1, keepdims=True)
    return values * lax.rsqrt(mean_square + epsilon) * gain_vector


def shards(
    support_tokens,
    support_lengths,
    support_labels,
    query_tokens,
    query_lengths,
    query_episodes,
    embedding,
    attn_gain,
    query_weight,
    key_weight,
    value_weight,
    out_weight,
    final_gain,
):
    group_count = lax.axis_size(("dp", "pipe"))
    sections = lax.axis_size("pipe")
    sup_dev, seq_len = support_tokens.shape
    qry_dev = query_tokens.shape[0]
    seq_count = sup_dev + qry_dev
    row_count = seq_count * seq_len
    table_rows, width = embedding.shape
    column_start = lax.axis_index("tensor") * width
    all_support, all_query, every_sup_len, every_qry_len = (
        lax.all_gather(support_tokens, ("dp", "pipe"), axis=0, tiled=True),
        lax.all_gather(query_tokens, ("dp", "pipe"), axis=0, tiled=True),
        lax.all_gather(support_lengths, ("dp", "pipe"), axis=0, tiled=True),
        lax.all_gather(query_lengths, ("dp", "pipe"), axis=0, tiled=True),
    )
    token_flat = jnp.concatenate(
        [all_support.reshape(group_count, sup_dev * seq_len), all_query], axis=1
    ).reshape(group_count * row_count)
    local_ids = token_flat - lax.axis_index(("dp", "pipe")) * table_rows
    inside = (local_ids >= 0) & (local_ids < table_rows)
    picked = jnp.take(embedding, jnp.clip(local_ids, 0, table_rows - 1), axis=0)
    picked = jnp.where(inside[:, None], picked, jnp.zeros_like(picked))
    hidden = lax.psum_scatter(
        picked.astype(jnp.float32).astype(jnp.bfloat16),
        ("dp", "pipe"),
        scatter_dimension=0,
        tiled=True,
    )
    seq_lengths = jnp.concatenate([support_lengths, query_lengths], axis=0)
    query_proj = query_weight[0]
    key_proj = key_weight[0]
    value_proj = value_weight[0]
    out_proj = out_weight[0]
    gain_vector = attn_gain[0]
    local_heads = query_proj.shape[1] // HEAD_DIM
    local_groups = key_proj.shape[1] // HEAD_DIM
    group_size = local_heads // local_groups
    w_in = jnp.concatenate([query_proj, key_proj, value_proj], axis=1)
    query_cols = local_heads * HEAD_DIM
    key_cols = local_groups * HEAD_DIM
    positions = jnp.arange(seq_len)
    causal = positions[None, :] <= positions[:, None]

    def section_block(stream, lengths_here):
        normed = whole_values(whole_rows(stream), gain_vector).astype(jnp.bfloat16)
        projected = jnp.dot(normed, w_in, preferred_element_type=jnp.float32)
        query_heads = projected[:, :query_cols].reshape(seq_count, seq_len, local_heads, HEAD_DIM)
        key_heads = projected[:, query_cols : query_cols + key_cols].reshape(
            seq_count, seq_len, local_groups, HEAD_DIM
        )
        value_heads = (
            projected[:, query_cols + key_cols :]
            .reshape(seq_count, seq_len, local_groups, HEAD_DIM)
            .astype(jnp.bfloat16)
        )
        query_heads = (
            rotate(query_heads, seq_len)
            .astype(jnp.bfloat16)
            .reshape(seq_count, seq_len, local_groups, group_size, HEAD_DIM)
        )
        key_heads = rotate(key_heads, seq_len).astype(jnp.bfloat16)
        scores = jnp.einsum(
            "sikgd,sjkd->skgij", query_heads, key_heads, preferred_element_type=jnp.float32
        ) / math.sqrt(HEAD_DIM)
        visible = causal[None, :, :] & (positions[None, None, :] < lengths_here[:, None, None])
        scores = jnp.where(visible[:, None, None, :, :], scores, -1e30)
        weights = jax.nn.softmax(scores, axis=-1).astype(jnp.bfloat16)
        mixed = jnp.einsum(
            "skgij,sjkd->sikgd", weights, value_heads, preferred_element_type=jnp.float32
        )
        mixed = mixed.astype(jnp.bfloat16).reshape(row_count, query_cols)
        partial_out = jnp.dot(mixed, out_proj, preferred_element_type=jnp.float32)
        summed = lax.psum_scatter(
            partial_out.astype(jnp.bfloat16), "tensor", scatter_dimension=1, tiled=True
        ).astype(jnp.float32)
        return (stream.astype(jnp.float32) + summed).astype(jnp.bfloat16)

    section_index = lax.axis_index("pipe")
    dp_base = lax.axis_index("dp") * sections

    def tick(tick_index, stream):
        held_group = dp_base + (section_index - tick_index) % sections
        sup_part = lax.dynamic_slice_in_dim(every_sup_len, held_group * sup_dev, sup_dev)
        qry_part = lax.dynamic_slice_in_dim(every_qry_len, held_group * qry_dev, qry_dev)
        lengths_here = jnp.concatenate([sup_part, qry_part], axis=0)
        first_tick = (tick_index - section_index) % sections
        active = (first_tick <= tick_index) & (tick_index < first_tick + sections)
        computed = section_block(stream, lengths_here)
        stream = jnp.where(active, computed, stream)
        return passed_along(stream, "pipe", 1)

    hidden = lax.fori_loop(0, 2 * sections, tick, hidden)
    final = lax.dynamic_slice_in_dim(
        whole_values(whole_rows(hidden), final_gain), column_start, width, 1
    )
    live = (positions[None, :] < seq_lengths[:, None]).astype(jnp.float32)
    pooled = jnp.sum(
        final.reshape(seq_count, seq_len, width) * live[:, :, None], axis=1
    ) / seq_lengths[:, None].astype(jnp.float32)
    support_pooled = pooled[:sup_dev]
    query_pooled = pooled[sup_dev:]
    class_count_all = EPISODES * WAYS
    onehot = (support_labels[:, 0][:, None] == jnp.arange(class_count_all)[None, :]).astype(
        jnp.float32
    )
    class_total = jnp.dot(onehot.T, support_pooled, precision=lax.Precision.HIGHEST)
    class_count = jnp.sum(onehot, axis=0)
    class_total, class_count = (
        lax.psum(class_total.astype(jnp.bfloat16), ("dp", "pipe")).astype(jnp.float32),
        lax.psum(class_count.astype(jnp.bfloat16), ("dp", "pipe")).astype(jnp.float32),
    )
    prototypes = class_total / class_count[:, None]
    episode_pick = (query_episodes[:, None] == jnp.arange(EPISODES)[None, :]).astype(jnp.float32)
    chosen = jnp.einsum(
        "qe,ewc->qwc",
        episode_pick,
        prototypes.reshape(EPISODES, WAYS, width),
        precision=lax.Precision.HIGHEST,
    )
    partial_distance = jnp.sum((query_pooled[:, None, :] - chosen) ** 2, axis=-1)
    distance = lax.psum(partial_distance, "tensor")
    logits = -distance / math.sqrt(D)
    return (prototypes, logits)


def solution(mesh):
    return jax.shard_map(
        shards,
        mesh=mesh,
        in_specs=(
            P(("dp", "pipe"), None),
            P(("dp", "pipe")),
            P(("dp", "pipe"), None),
            P(("dp", "pipe"), None),
            P(("dp", "pipe")),
            P(("dp", "pipe")),
            P(("dp", "pipe"), "tensor"),
            P("pipe", None),
            P("pipe", None, "tensor"),
            P("pipe", None, "tensor"),
            P("pipe", None, "tensor"),
            P("pipe", "tensor", None),
            P(),
        ),
        out_specs=(P(None, "tensor"), P(("dp", "pipe"), None)),
        check_vma=False,
    )
```

profile of v0, /device:TPU:8, one launch (start us, length us, event | category | flops | bytes accessed | tf_op | source)
XLA Modules:
  0.0 830.7 jit_solution(18302538500788156600)
XLA Ops:
  7.2 29.0 %all-gather.1 = s32[16,1,32]{2,1,0:T(1,128)S(1)} all-gather(s32[1,1,32]{2,1,0:T(1,128)} %bitcast.117), channel_id=1, replica_groups=mesh['dp'=4,'pipe'=4,'tensor'=2] {'dp','pipe'}, dimensions={0}, use_global_device_ids=true | all-gather | bytes 2176 | tf_op jit(solution)/shard_map/all_gather | solution.py:72
  36.2 33.0 %all-gather = s32[16,2,32]{2,1,0:T(2,128)S(1)} all-gather(s32[1,2,32]{2,1,0:T(2,128)} %bitcast.113), channel_id=1, replica_groups=mesh['dp'=4,'pipe'=4,'tensor'=2] {'dp','pipe'}, dimensions={0}, use_global_device_ids=true | all-gather | bytes 4352 | tf_op jit(solution)/shard_map/all_gather | solution.py:71
  69.7 20.5 %gather_fusion = bf16[1536,2048]{1,0:T(8,128)(2,1)} fusion(bf16[4008,2048]{1,0:T(8,128)(2,1)} %param.21, s32[2048]{0:T(1024)S(1)} %pad_clamp_fusion), kind=kCustom, calls=%fused_computation | custom fusion | bytes 12589056 | tf_op jit(solution)/shard_map/jit(_take)/gather | solution.py:81
  108.2 18.7 %pad_maximum_fusion = bf16[4096,3072]{1,0:T(8,128)(2,1)} fusion(bf16[4096,512]{1,0:T(8,128)(2,1)} %bitcast.104, bf16[4096,512]{1,0:T(8,128)(2,1)} %bitcast.105, bf16[4096,2048]{1,0:T(8,128)(2,1)} %bitcast.99), kind=kLoop, calls=%fused_computation.54 | loop fusion | flops 75497472 | bytes 50331648 | tf_op jit(solution)/shard_map/concatenate | solution.py:98
  126.8 53.5 %reduce-scatter.3.cloned.1.call-done = bf16[96,2048]{1,0:T(8,128)(2,1)} async-done(((bf16[1536,2048]{1,0:T(8,128)(2,1)}), bf16[96,2048]{1,0:T(8,128)(2,1)}) %reduce-scatter.3.cloned.1.call-update) | async-done | bytes 393232 | tf_op jit(solution)/shard_map/reduce_scatter | solution.py:83
  180.3 532.5 %while.16 = (s32[]{:T(128)}, bf16[96,2048]{1,0:T(8,128)(2,1)}, s32[]{:T(128)}, f32[1,4096]{1,0:T(1,128)S(1)}, bf16[4096,3072]{1,0:T(8,128)(2,1)}, /*index=5*/s32...) while((s32[]{:T(128)}, bf16[96,2048]{1,0:T(8,128)(2,1)}, ...), condition=%wide.region_6.7_spmd.clone, body=%wide.region_1.0_spmd.clone.sunk | while | flops 4072005120 | bytes 66611072 | solution.py:152
  180.4 11.0 %all_gather.32 = bf16[96,4096]{1,0:T(8,128)(2,1)S(1)} all-gather(bf16[96,2048]{1,0:T(8,128)(2,1)} %get-tuple-element.408), channel_id=1, replica_groups=mesh['dp'=4,'pipe'=4,'tensor'=2] {'tensor'}, dimensions={1}, use_global_device_ids=true | all-gather | bytes 1179648 | tf_op jit(solution)/shard_map/while/body/eval_jaxpr/all_gather | solution.py:38
  216.9 17.6 %reduce-scatter.5.cloned.1.call-done = bf16[96,2048]{1,0:T(8,128)(2,1)} async-done(((bf16[96,4096]{1,0:T(8,128)(2,1)}), bf16[96,2048]{1,0:T(8,128)(2,1)}) %reduce-scatter.5.cloned.1.call-update) | async-done | bytes 393232 | tf_op jit(solution)/shard_map/while/body/eval_jaxpr/reduce_scatter | solution.py:133
  247.2 10.7 %all_gather.32 = bf16[96,4096]{1,0:T(8,128)(2,1)S(1)} all-gather(bf16[96,2048]{1,0:T(8,128)(2,1)} %get-tuple-element.408), channel_id=1, replica_groups=mesh['dp'=4,'pipe'=4,'tensor'=2] {'tensor'}, dimensions={1}, use_global_device_ids=true | all-gather | bytes 1179648 | tf_op jit(solution)/shard_map/while/body/eval_jaxpr/all_gather | solution.py:38
  283.4 17.6 %reduce-scatter.5.cloned.1.call-done = bf16[96,2048]{1,0:T(8,128)(2,1)} async-done(((bf16[96,4096]{1,0:T(8,128)(2,1)}), bf16[96,2048]{1,0:T(8,128)(2,1)}) %reduce-scatter.5.cloned.1.call-update) | async-done | bytes 393232 | tf_op jit(solution)/shard_map/while/body/eval_jaxpr/reduce_scatter | solution.py:133
  313.7 10.7 %all_gather.32 = bf16[96,4096]{1,0:T(8,128)(2,1)S(1)} all-gather(bf16[96,2048]{1,0:T(8,128)(2,1)} %get-tuple-element.408), channel_id=1, replica_groups=mesh['dp'=4,'pipe'=4,'tensor'=2] {'tensor'}, dimensions={1}, use_global_device_ids=true | all-gather | bytes 1179648 | tf_op jit(solution)/shard_map/while/body/eval_jaxpr/all_gather | solution.py:38
  349.9 17.7 %reduce-scatter.5.cloned.1.call-done = bf16[96,2048]{1,0:T(8,128)(2,1)} async-done(((bf16[96,4096]{1,0:T(8,128)(2,1)}), bf16[96,2048]{1,0:T(8,128)(2,1)}) %reduce-scatter.5.cloned.1.call-update) | async-done | bytes 393232 | tf_op jit(solution)/shard_map/while/body/eval_jaxpr/reduce_scatter | solution.py:133
  416.4 17.6 %reduce-scatter.5.cloned.1.call-done = bf16[96,2048]{1,0:T(8,128)(2,1)} async-done(((bf16[96,4096]{1,0:T(8,128)(2,1)}), bf16[96,2048]{1,0:T(8,128)(2,1)}) %reduce-scatter.5.cloned.1.call-update) | async-done | bytes 393232 | tf_op jit(solution)/shard_map/while/body/eval_jaxpr/reduce_scatter | solution.py:133
  446.7 10.7 %all_gather.32 = bf16[96,4096]{1,0:T(8,128)(2,1)S(1)} all-gather(bf16[96,2048]{1,0:T(8,128)(2,1)} %get-tuple-element.408), channel_id=1, replica_groups=mesh['dp'=4,'pipe'=4,'tensor'=2] {'tensor'}, dimensions={1}, use_global_device_ids=true | all-gather | bytes 1179648 | tf_op jit(solution)/shard_map/while/body/eval_jaxpr/all_gather | solution.py:38
  483.0 17.6 %reduce-scatter.5.cloned.1.call-done = bf16[96,2048]{1,0:T(8,128)(2,1)} async-done(((bf16[96,4096]{1,0:T(8,128)(2,1)}), bf16[96,2048]{1,0:T(8,128)(2,1)}) %reduce-scatter.5.cloned.1.call-update) | async-done | bytes 393232 | tf_op jit(solution)/shard_map/while/body/eval_jaxpr/reduce_scatter | solution.py:133
  513.3 10.7 %all_gather.32 = bf16[96,4096]{1,0:T(8,128)(2,1)S(1)} all-gather(bf16[96,2048]{1,0:T(8,128)(2,1)} %get-tuple-element.408), channel_id=1, replica_groups=mesh['dp'=4,'pipe'=4,'tensor'=2] {'tensor'}, dimensions={1}, use_global_device_ids=true | all-gather | bytes 1179648 | tf_op jit(solution)/shard_map/while/body/eval_jaxpr/all_gather | solution.py:38
  549.5 17.6 %reduce-scatter.5.cloned.1.call-done = bf16[96,2048]{1,0:T(8,128)(2,1)} async-done(((bf16[96,4096]{1,0:T(8,128)(2,1)}), bf16[96,2048]{1,0:T(8,128)(2,1)}) %reduce-scatter.5.cloned.1.call-update) | async-done | bytes 393232 | tf_op jit(solution)/shard_map/while/body/eval_jaxpr/reduce_scatter | solution.py:133
  579.8 10.7 %all_gather.32 = bf16[96,4096]{1,0:T(8,128)(2,1)S(1)} all-gather(bf16[96,2048]{1,0:T(8,128)(2,1)} %get-tuple-element.408), channel_id=1, replica_groups=mesh['dp'=4,'pipe'=4,'tensor'=2] {'tensor'}, dimensions={1}, use_global_device_ids=true | all-gather | bytes 1179648 | tf_op jit(solution)/shard_map/while/body/eval_jaxpr/all_gather | solution.py:38
  616.0 17.6 %reduce-scatter.5.cloned.1.call-done = bf16[96,2048]{1,0:T(8,128)(2,1)} async-done(((bf16[96,4096]{1,0:T(8,128)(2,1)}), bf16[96,2048]{1,0:T(8,128)(2,1)}) %reduce-scatter.5.cloned.1.call-update) | async-done | bytes 393232 | tf_op jit(solution)/shard_map/while/body/eval_jaxpr/reduce_scatter | solution.py:133
  646.3 10.7 %all_gather.32 = bf16[96,4096]{1,0:T(8,128)(2,1)S(1)} all-gather(bf16[96,2048]{1,0:T(8,128)(2,1)} %get-tuple-element.408), channel_id=1, replica_groups=mesh['dp'=4,'pipe'=4,'tensor'=2] {'tensor'}, dimensions={1}, use_global_device_ids=true | all-gather | bytes 1179648 | tf_op jit(solution)/shard_map/while/body/eval_jaxpr/all_gather | solution.py:38
  682.5 17.6 %reduce-scatter.5.cloned.1.call-done = bf16[96,2048]{1,0:T(8,128)(2,1)} async-done(((bf16[96,4096]{1,0:T(8,128)(2,1)}), bf16[96,2048]{1,0:T(8,128)(2,1)}) %reduce-scatter.5.cloned.1.call-update) | async-done | bytes 393232 | tf_op jit(solution)/shard_map/while/body/eval_jaxpr/reduce_scatter | solution.py:133
  712.8 10.8 %all_gather.29 = bf16[96,4096]{1,0:T(8,128)(2,1)S(1)} all-gather(bf16[96,2048]{1,0:T(8,128)(2,1)} %get-tuple-element.268), channel_id=1, replica_groups=mesh['dp'=4,'pipe'=4,'tensor'=2] {'tensor'}, dimensions={1}, use_global_device_ids=true | all-gather | bytes 1179648 | tf_op jit(solution)/shard_map/all_gather | solution.py:38
  725.6 32.3 %psum.22 = bf16[32]{0:T(256)(128)(2,1)S(1)} all-reduce(bf16[32]{0:T(256)(128)(2,1)S(1)} %convert_reduce_fusion), channel_id=1, replica_groups=mesh['dp'=4,'pipe'=4,'tensor'=2] {'dp','pipe'}, use_global_device_ids=true, to_apply=%region_11.12 | all-reduce | flops 32 | bytes 128 | tf_op jit(solution)/shard_map/psum | solution.py:170
  758.6 57.9 %all-reduce.5.cloned.1.call-done = bf16[32,2048]{1,0:T(8,128)(2,1)} async-done(((bf16[32,2048]{1,0:T(8,128)(2,1)}), bf16[32,2048]{1,0:T(8,128)(2,1)}) %all-reduce.5.cloned.1.call-update) | async-done | bytes 131088 | tf_op jit(solution)/shard_map/psum | solution.py:169
  (338 shorter events, 341.1 us)
Async XLA Ops:
  7.2 173.2 %reduce-scatter.3.cloned.1.call-start = ((), (), s32[]{:S(2)}) async-start(), calls=%async_computation.2 | async-start | bytes 6684672 | tf_op jit(solution)/shard_map/reduce_scatter | solution.py:83
  108.2 72.1 %copy-start.2 = (f32[1,4096]{1,0:T(1,128)S(1)}, f32[1,4096]{1,0:T(1,128)}, u32[]{:S(2)}) copy-start(f32[1,4096]{1,0:T(1,128)} %param.22) | copy-start | bytes 49156
  180.3 543.7 %dynamic-slice-start = ((f32[4096]{0:T(1024)}, s32[]{:T(128)}), f32[2048]{0:T(1024)S(1)}, s32[]{:S(2)}) async-start(f32[4096]{0:T(1024)} %param.27, s32[]{:T(128)} %select_n.115), calls=%async_computation.5 | async-start | bytes 16896 | tf_op jit(solution)/shard_map/dynamic_slice | solution.py:153
  180.3 54.2 %reduce-scatter.5.cloned.1.call-start = ((), (), s32[]{:S(2)}) async-start(), calls=%async_computation.4 | async-start | bytes 1179648 | tf_op jit(solution)/shard_map/while/body/eval_jaxpr/reduce_scatter | solution.py:133
  235.6 10.8 %collective-permute-start = (bf16[96,2048]{1,0:T(8,128)(2,1)S(1)}, bf16[96,2048]{1,0:T(8,128)(2,1)S(1)}, u32[]{:S(2)}, u32[]{:S(2)}) collective-permute-start(bf16[96,2048]{1,0:T(8,128)(2,1)S(1)} %fusion.94), channel_id=1, source_target_pairs={{6,0},{0,2},{2,4},{4,6},{7,1},{1,3},{3,5},{5,7},{14,8},{8,10},{10,... | collective-permute-start | bytes 1179656 | tf_op jit(solution)/shard_map/while/body/eval_jaxpr/ppermute | solution.py:18
  247.1 53.9 %reduce-scatter.5.cloned.1.call-start = ((), (), s32[]{:S(2)}) async-start(), calls=%async_computation.4 | async-start | bytes 1179648 | tf_op jit(solution)/shard_map/while/body/eval_jaxpr/reduce_scatter | solution.py:133
  302.1 10.7 %collective-permute-start = (bf16[96,2048]{1,0:T(8,128)(2,1)S(1)}, bf16[96,2048]{1,0:T(8,128)(2,1)S(1)}, u32[]{:S(2)}, u32[]{:S(2)}) collective-permute-start(bf16[96,2048]{1,0:T(8,128)(2,1)S(1)} %fusion.94), channel_id=1, source_target_pairs={{6,0},{0,2},{2,4},{4,6},{7,1},{1,3},{3,5},{5,7},{14,8},{8,10},{10,... | collective-permute-start | bytes 1179656 | tf_op jit(solution)/shard_map/while/body/eval_jaxpr/ppermute | solution.py:18
  313.6 53.9 %reduce-scatter.5.cloned.1.call-start = ((), (), s32[]{:S(2)}) async-start(), calls=%async_computation.4 | async-start | bytes 1179648 | tf_op jit(solution)/shard_map/while/body/eval_jaxpr/reduce_scatter | solution.py:133
  340.3 27.3 %copy-start = (bf16[96,2048]{1,0:T(8,128)(2,1)S(1)}, bf16[96,2048]{1,0:T(8,128)(2,1)}, u32[]{:S(2)}) copy-start(bf16[96,2048]{1,0:T(8,128)(2,1)} %get-tuple-element.408) | copy-start | bytes 1179652 | tf_op jit(solution)/shard_map/while
  368.7 10.7 %collective-permute-start = (bf16[96,2048]{1,0:T(8,128)(2,1)S(1)}, bf16[96,2048]{1,0:T(8,128)(2,1)S(1)}, u32[]{:S(2)}, u32[]{:S(2)}) collective-permute-start(bf16[96,2048]{1,0:T(8,128)(2,1)S(1)} %fusion.94), channel_id=1, source_target_pairs={{6,0},{0,2},{2,4},{4,6},{7,1},{1,3},{3,5},{5,7},{14,8},{8,10},{10,... | collective-permute-start | bytes 1179656 | tf_op jit(solution)/shard_map/while/body/eval_jaxpr/ppermute | solution.py:18
  380.2 53.9 %reduce-scatter.5.cloned.1.call-start = ((), (), s32[]{:S(2)}) async-start(), calls=%async_computation.4 | async-start | bytes 1179648 | tf_op jit(solution)/shard_map/while/body/eval_jaxpr/reduce_scatter | solution.py:133
  406.8 27.2 %copy-start = (bf16[96,2048]{1,0:T(8,128)(2,1)S(1)}, bf16[96,2048]{1,0:T(8,128)(2,1)}, u32[]{:S(2)}) copy-start(bf16[96,2048]{1,0:T(8,128)(2,1)} %get-tuple-element.408) | copy-start | bytes 1179652 | tf_op jit(solution)/shard_map/while
  435.2 10.8 %collective-permute-start = (bf16[96,2048]{1,0:T(8,128)(2,1)S(1)}, bf16[96,2048]{1,0:T(8,128)(2,1)S(1)}, u32[]{:S(2)}, u32[]{:S(2)}) collective-permute-start(bf16[96,2048]{1,0:T(8,128)(2,1)S(1)} %fusion.94), channel_id=1, source_target_pairs={{6,0},{0,2},{2,4},{4,6},{7,1},{1,3},{3,5},{5,7},{14,8},{8,10},{10,... | collective-permute-start | bytes 1179656 | tf_op jit(solution)/shard_map/while/body/eval_jaxpr/ppermute | solution.py:18
  446.7 53.9 %reduce-scatter.5.cloned.1.call-start = ((), (), s32[]{:S(2)}) async-start(), calls=%async_computation.4 | async-start | bytes 1179648 | tf_op jit(solution)/shard_map/while/body/eval_jaxpr/reduce_scatter | solution.py:133
  473.4 27.2 %copy-start = (bf16[96,2048]{1,0:T(8,128)(2,1)S(1)}, bf16[96,2048]{1,0:T(8,128)(2,1)}, u32[]{:S(2)}) copy-start(bf16[96,2048]{1,0:T(8,128)(2,1)} %get-tuple-element.408) | copy-start | bytes 1179652 | tf_op jit(solution)/shard_map/while
  501.7 10.7 %collective-permute-start = (bf16[96,2048]{1,0:T(8,128)(2,1)S(1)}, bf16[96,2048]{1,0:T(8,128)(2,1)S(1)}, u32[]{:S(2)}, u32[]{:S(2)}) collective-permute-start(bf16[96,2048]{1,0:T(8,128)(2,1)S(1)} %fusion.94), channel_id=1, source_target_pairs={{6,0},{0,2},{2,4},{4,6},{7,1},{1,3},{3,5},{5,7},{14,8},{8,10},{10,... | collective-permute-start | bytes 1179656 | tf_op jit(solution)/shard_map/while/body/eval_jaxpr/ppermute | solution.py:18
  513.2 53.9 %reduce-scatter.5.cloned.1.call-start = ((), (), s32[]{:S(2)}) async-start(), calls=%async_computation.4 | async-start | bytes 1179648 | tf_op jit(solution)/shard_map/while/body/eval_jaxpr/reduce_scatter | solution.py:133
  539.9 27.2 %copy-start = (bf16[96,2048]{1,0:T(8,128)(2,1)S(1)}, bf16[96,2048]{1,0:T(8,128)(2,1)}, u32[]{:S(2)}) copy-start(bf16[96,2048]{1,0:T(8,128)(2,1)} %get-tuple-element.408) | copy-start | bytes 1179652 | tf_op jit(solution)/shard_map/while
  568.2 10.8 %collective-permute-start = (bf16[96,2048]{1,0:T(8,128)(2,1)S(1)}, bf16[96,2048]{1,0:T(8,128)(2,1)S(1)}, u32[]{:S(2)}, u32[]{:S(2)}) collective-permute-start(bf16[96,2048]{1,0:T(8,128)(2,1)S(1)} %fusion.94), channel_id=1, source_target_pairs={{6,0},{0,2},{2,4},{4,6},{7,1},{1,3},{3,5},{5,7},{14,8},{8,10},{10,... | collective-permute-start | bytes 1179656 | tf_op jit(solution)/shard_map/while/body/eval_jaxpr/ppermute | solution.py:18
  579.8 53.8 %reduce-scatter.5.cloned.1.call-start = ((), (), s32[]{:S(2)}) async-start(), calls=%async_computation.4 | async-start | bytes 1179648 | tf_op jit(solution)/shard_map/while/body/eval_jaxpr/reduce_scatter | solution.py:133
  634.8 10.8 %collective-permute-start = (bf16[96,2048]{1,0:T(8,128)(2,1)S(1)}, bf16[96,2048]{1,0:T(8,128)(2,1)S(1)}, u32[]{:S(2)}, u32[]{:S(2)}) collective-permute-start(bf16[96,2048]{1,0:T(8,128)(2,1)S(1)} %fusion.94), channel_id=1, source_target_pairs={{6,0},{0,2},{2,4},{4,6},{7,1},{1,3},{3,5},{5,7},{14,8},{8,10},{10,... | collective-permute-start | bytes 1179656 | tf_op jit(solution)/shard_map/while/body/eval_jaxpr/ppermute | solution.py:18
  646.3 53.9 %reduce-scatter.5.cloned.1.call-start = ((), (), s32[]{:S(2)}) async-start(), calls=%async_computation.4 | async-start | bytes 1179648 | tf_op jit(solution)/shard_map/while/body/eval_jaxpr/reduce_scatter | solution.py:133
  701.3 10.7 %collective-permute-start = (bf16[96,2048]{1,0:T(8,128)(2,1)S(1)}, bf16[96,2048]{1,0:T(8,128)(2,1)S(1)}, u32[]{:S(2)}, u32[]{:S(2)}) collective-permute-start(bf16[96,2048]{1,0:T(8,128)(2,1)S(1)} %fusion.94), channel_id=1, source_target_pairs={{6,0},{0,2},{2,4},{4,6},{7,1},{1,3},{3,5},{5,7},{14,8},{8,10},{10,... | collective-permute-start | bytes 1179656 | tf_op jit(solution)/shard_map/while/body/eval_jaxpr/ppermute | solution.py:18
  712.8 103.8 %all-reduce.5.cloned.1.call-start = ((), (), s32[]{:S(2)}) async-start(), calls=%async_computation.3 | async-start | bytes 262144 | tf_op jit(solution)/shard_map/psum | solution.py:169
  (16 other events, 135.7 us)
Sparse Core Ops, SparseCore 0:
  97.4 82.8 reduce-scatter.2
  217.0 17.4 reduce-scatter.4
  283.5 17.4 reduce-scatter.4
  350.0 17.5 reduce-scatter.4
  416.5 17.4 reduce-scatter.4
  483.1 17.5 reduce-scatter.4
  549.6 17.4 reduce-scatter.4
  616.1 17.4 reduce-scatter.4
  682.6 17.4 reduce-scatter.4
  725.7 90.8 all-reduce.4
where the time goes:
time: 832 us; the launch traced here: 831 us
  waiting for transfers between devices  326 us (39%)
  blocking collectives  204 us (25%)
  matrix products  177 us (21%)
  other arithmetic  50.2 us (6%)
  local copies, waits for them, and re-layouts  43.8 us (5%)
  between operations  16.2 us (2%)
  starting transfers between devices  12.4 us (1%)
    reduce_scatter x8, waiting for transfers between devices, section_block(): lax.psum_scatter(partial_out.astype(jnp.bfloat16), 'tensor', scatter_dime...  141 us
    all_gather x9, blocking collectives, whole_rows(): return lax.all_gather(hidden, 'tensor', axis=1, tiled=True)  96.8 us
    dot_general x8, matrix products, section_block(): projected = jnp.dot(normed, w_in, preferred_element_type=jnp.float32)  83.3 us
    dot_general x8, matrix products, section_block(): partial_out = jnp.dot(mixed, out_proj, preferred_element_type=jnp.float32)  76.2 us
    ppermute x8, waiting for transfers between devices, passed_along(): return lax.ppermute(block, axis, route)  73.6 us
    psum x1, waiting for transfers between devices, shards(): lax.psum(class_total.astype(jnp.bfloat16), ('dp', 'pipe'))  57.9 us
    reduce_scatter x1, waiting for transfers between devices, shards(): lax.psum_scatter(picked.astype(jnp.float32).astype(jnp.bfloat16), ('dp',...  53.5 us
    all_gather x1, blocking collectives, shards(): lax.all_gather(support_tokens, ('dp', 'pipe'), axis=0, tiled=True)  33 us
  transfers between devices with their start and end apart: 18, of which 18 were waited for; matrix products, arithmetic and copies ran while one was open for 2% of the time, Pallas kernels for 0%

commit v1 on v0

--- a/solution.py
+++ b/solution.py
@@ -35,7 +35,15 @@
 
 
 def whole_rows(hidden):
-    return lax.all_gather(hidden, "tensor", axis=1, tiled=True)
+    return jnp.concatenate(
+        lax.all_to_all(
+            jnp.stack([hidden] * lax.axis_size("tensor")),
+            axis_name="tensor",
+            split_axis=0,
+            concat_axis=0,
+        ),
+        axis=1,
+    )
 
 
 def whole_values(full_rows, gain_vector):

time: 832 us -> 865 us (1.040)
  blocking collectives: 204 us -> 107 us
  waiting for transfers between devices: 326 us -> 402 us
  starting transfers between devices: 12.4 us -> 44.4 us
  other arithmetic: 50.2 us -> 70.5 us
    all_gather x9 -> x0, blocking collectives: 96.8 us -> none  [whole_rows(): return lax.all_gather(hidden, 'tensor', axis=1, tiled=True)]
    all_to_all x0 -> x9, waiting for transfers between devices: none -> 76.3 us  [whole_rows(): lax.all_to_all(jnp.stack([hidden] * lax.axis_size('tensor')), axis_name='...]
    all_to_all x0 -> x9, starting transfers between devices: none -> 31.8 us  [whole_rows(): lax.all_to_all(jnp.stack([hidden] * lax.axis_size('tensor')), axis_name='...]
    another operation x16 -> x25, other arithmetic: 3 us -> 22.1 us  [the longest x9 19.1 us: whole_rows(): jnp.stack([hidden] * lax.axis_size('tensor'))]
  transfers between devices with their start and end apart: 18 -> 27, of which waited for: 18 -> 27; matrix products, arithmetic and copies ran while one was open for 2% -> 4% of each run, Pallas kernels for 0% -> 0%
where the time goes in v1:
time: 865 us; the launch traced here: 864 us
  waiting for transfers between devices  402 us (46%)
  matrix products  177 us (20%)
  blocking collectives  107 us (12%)
  other arithmetic  70.5 us (8%)
  local copies, waits for them, and re-layouts  45.3 us (5%)
  starting transfers between devices  44.4 us (5%)
  between operations  16.2 us (2%)
    reduce_scatter x8, waiting for transfers between devices, section_block(): lax.psum_scatter(partial_out.astype(jnp.bfloat16), 'tensor', scatter_dime...  140 us
    dot_general x8, matrix products, section_block(): projected = jnp.dot(normed, w_in, preferred_element_type=jnp.float32)  83.1 us
    all_to_all x9, waiting for transfers between devices, whole_rows(): lax.all_to_all(jnp.stack([hidden] * lax.axis_size('tensor')), axis_name='...  76.3 us
    dot_general x8, matrix products, section_block(): partial_out = jnp.dot(mixed, out_proj, preferred_element_type=jnp.float32)  76.2 us
    ppermute x8, waiting for transfers between devices, passed_along(): return lax.ppermute(block, axis, route)  73.6 us
    psum x1, waiting for transfers between devices, shards(): lax.psum(class_total.astype(jnp.bfloat16), ('dp', 'pipe'))  58 us
    reduce_scatter x1, waiting for transfers between devices, shards(): lax.psum_scatter(picked.astype(jnp.float32).astype(jnp.bfloat16), ('dp',...  53.6 us
    all_gather x1, blocking collectives, shards(): lax.all_gather(support_tokens, ('dp', 'pipe'), axis=0, tiled=True)  33 us
  transfers between devices with their start and end apart: 27, of which 27 were waited for; matrix products, arithmetic and copies ran while one was open for 4% of the time, Pallas kernels for 0%

profile of v1, /device:TPU:8, one launch (start us, length us, event | category | flops | bytes accessed | tf_op | source)
XLA Modules:
  0.0 863.8 jit_solution(1801952941537797524)
XLA Ops:
  7.2 29.0 %all-gather.1 = s32[16,1,32]{2,1,0:T(1,128)S(1)} all-gather(s32[1,1,32]{2,1,0:T(1,128)} %bitcast.137), channel_id=1, replica_groups=mesh['dp'=4,'pipe'=4,'tensor'=2] {'dp','pipe'}, dimensions={0}, use_global_device_ids=true | all-gather | bytes 2176 | tf_op jit(solution)/shard_map/all_gather | solution.py:80
  36.2 33.0 %all-gather = s32[16,2,32]{2,1,0:T(2,128)S(1)} all-gather(s32[1,2,32]{2,1,0:T(2,128)} %bitcast.133), channel_id=1, replica_groups=mesh['dp'=4,'pipe'=4,'tensor'=2] {'dp','pipe'}, dimensions={0}, use_global_device_ids=true | all-gather | bytes 4352 | tf_op jit(solution)/shard_map/all_gather | solution.py:79
  69.7 20.5 %gather_fusion = bf16[1536,2048]{1,0:T(8,128)(2,1)} fusion(bf16[4008,2048]{1,0:T(8,128)(2,1)} %param.21, s32[2048]{0:T(1024)S(1)} %pad_clamp_fusion), kind=kCustom, calls=%fused_computation | custom fusion | bytes 12589056 | tf_op jit(solution)/shard_map/jit(_take)/gather | solution.py:89
  108.0 18.6 %pad_maximum_fusion.1 = bf16[4096,3072]{1,0:T(8,128)(2,1)} fusion(bf16[4096,512]{1,0:T(8,128)(2,1)} %bitcast.123, bf16[4096,512]{1,0:T(8,128)(2,1)} %bitcast.124, bf16[4096,2048]{1,0:T(8,128)(2,1)} %bitcast.118), kind=kLoop, calls=%fused_computation.54 | loop fusion | flops 75497472 | bytes 50331648 | tf_op jit(solution)/shard_map/concatenate | solution.py:106
  126.7 53.6 %reduce-scatter.3.cloned.1.call-done = bf16[96,2048]{1,0:T(8,128)(2,1)} async-done(((bf16[1536,2048]{1,0:T(8,128)(2,1)}), bf16[96,2048]{1,0:T(8,128)(2,1)}) %reduce-scatter.3.cloned.1.call-update) | async-done | bytes 393232 | tf_op jit(solution)/shard_map/reduce_scatter | solution.py:91
  180.3 560.5 %while.16 = (s32[]{:T(128)}, bf16[96,2048]{1,0:T(8,128)(2,1)}, s32[]{:T(128)}, f32[1,4096]{1,0:T(1,128)S(1)}, bf16[4096,3072]{1,0:T(8,128)(2,1)}, /*index=5*/s32...) while((s32[]{:T(128)}, bf16[96,2048]{1,0:T(8,128)(2,1)}, ...), condition=%wide.region_6.7_spmd.clone, body=%wide.region_1.0_spmd.clone.sunk | while | flops 4072398336 | bytes 75261856 | solution.py:160
  196.9 10.4 %fusion.85 = f32[96,3072]{1,0:T(8,128)S(1)} fusion(bf16[4096,3072]{1,0:T(8,128)(2,1)} %get-tuple-element.427, f32[96,4096]{1,0:T(8,128)S(1)} %bitcast.114, f32[4096]{0:T(1024)S(1)} %bitcast.128, f32[96]{0:T(128)S(1)} %add_rsqrt_fusion.3), kind=kOutput, calls=%fused_computation.16.clone.1 | convolution fusion | flops 2417098752 | bytes 27935104 | tf_op jit(solution)/shard_map/while/body/eval_jaxpr/dot_general | solution.py:114
  220.5 16.7 %reduce-scatter.5.cloned.1.call-done = bf16[96,2048]{1,0:T(8,128)(2,1)} async-done(((bf16[96,4096]{1,0:T(8,128)(2,1)}), bf16[96,2048]{1,0:T(8,128)(2,1)}) %reduce-scatter.5.cloned.1.call-update) | async-done | bytes 393232 | tf_op jit(solution)/shard_map/while/body/eval_jaxpr/reduce_scatter | solution.py:141
  266.1 10.4 %fusion.85 = f32[96,3072]{1,0:T(8,128)S(1)} fusion(bf16[4096,3072]{1,0:T(8,128)(2,1)} %get-tuple-element.427, f32[96,4096]{1,0:T(8,128)S(1)} %bitcast.114, f32[4096]{0:T(1024)S(1)} %bitcast.128, f32[96]{0:T(128)S(1)} %add_rsqrt_fusion.3), kind=kOutput, calls=%fused_computation.16.clone.1 | convolution fusion | flops 2417098752 | bytes 27935104 | tf_op jit(solution)/shard_map/while/body/eval_jaxpr/dot_general | solution.py:114
  289.7 17.6 %reduce-scatter.5.cloned.1.call-done = bf16[96,2048]{1,0:T(8,128)(2,1)} async-done(((bf16[96,4096]{1,0:T(8,128)(2,1)}), bf16[96,2048]{1,0:T(8,128)(2,1)}) %reduce-scatter.5.cloned.1.call-update) | async-done | bytes 393232 | tf_op jit(solution)/shard_map/while/body/eval_jaxpr/reduce_scatter | solution.py:141
  336.2 10.4 %fusion.85 = f32[96,3072]{1,0:T(8,128)S(1)} fusion(bf16[4096,3072]{1,0:T(8,128)(2,1)} %get-tuple-element.427, f32[96,4096]{1,0:T(8,128)S(1)} %bitcast.114, f32[4096]{0:T(1024)S(1)} %bitcast.128, f32[96]{0:T(128)S(1)} %add_rsqrt_fusion.3), kind=kOutput, calls=%fused_computation.16.clone.1 | convolution fusion | flops 2417098752 | bytes 27935104 | tf_op jit(solution)/shard_map/while/body/eval_jaxpr/dot_general | solution.py:114
  359.8 17.6 %reduce-scatter.5.cloned.1.call-done = bf16[96,2048]{1,0:T(8,128)(2,1)} async-done(((bf16[96,4096]{1,0:T(8,128)(2,1)}), bf16[96,2048]{1,0:T(8,128)(2,1)}) %reduce-scatter.5.cloned.1.call-update) | async-done | bytes 393232 | tf_op jit(solution)/shard_map/while/body/eval_jaxpr/reduce_scatter | solution.py:141
  406.4 10.4 %fusion.85 = f32[96,3072]{1,0:T(8,128)S(1)} fusion(bf16[4096,3072]{1,0:T(8,128)(2,1)} %get-tuple-element.427, f32[96,4096]{1,0:T(8,128)S(1)} %bitcast.114, f32[4096]{0:T(1024)S(1)} %bitcast.128, f32[96]{0:T(128)S(1)} %add_rsqrt_fusion.3), kind=kOutput, calls=%fused_computation.16.clone.1 | convolution fusion | flops 2417098752 | bytes 27935104 | tf_op jit(solution)/shard_map/while/body/eval_jaxpr/dot_general | solution.py:114
  430.0 17.6 %reduce-scatter.5.cloned.1.call-done = bf16[96,2048]{1,0:T(8,128)(2,1)} async-done(((bf16[96,4096]{1,0:T(8,128)(2,1)}), bf16[96,2048]{1,0:T(8,128)(2,1)}) %reduce-scatter.5.cloned.1.call-update) | async-done | bytes 393232 | tf_op jit(solution)/shard_map/while/body/eval_jaxpr/reduce_scatter | solution.py:141
  476.5 10.4 %fusion.85 = f32[96,3072]{1,0:T(8,128)S(1)} fusion(bf16[4096,3072]{1,0:T(8,128)(2,1)} %get-tuple-element.427, f32[96,4096]{1,0:T(8,128)S(1)} %bitcast.114, f32[4096]{0:T(1024)S(1)} %bitcast.128, f32[96]{0:T(128)S(1)} %add_rsqrt_fusion.3), kind=kOutput, calls=%fused_computation.16.clone.1 | convolution fusion | flops 2417098752 | bytes 27935104 | tf_op jit(solution)/shard_map/while/body/eval_jaxpr/dot_general | solution.py:114
  500.1 17.7 %reduce-scatter.5.cloned.1.call-done = bf16[96,2048]{1,0:T(8,128)(2,1)} async-done(((bf16[96,4096]{1,0:T(8,128)(2,1)}), bf16[96,2048]{1,0:T(8,128)(2,1)}) %reduce-scatter.5.cloned.1.call-update) | async-done | bytes 393232 | tf_op jit(solution)/shard_map/while/body/eval_jaxpr/reduce_scatter | solution.py:141
  546.6 10.4 %fusion.85 = f32[96,3072]{1,0:T(8,128)S(1)} fusion(bf16[4096,3072]{1,0:T(8,128)(2,1)} %get-tuple-element.427, f32[96,4096]{1,0:T(8,128)S(1)} %bitcast.114, f32[4096]{0:T(1024)S(1)} %bitcast.128, f32[96]{0:T(128)S(1)} %add_rsqrt_fusion.3), kind=kOutput, calls=%fused_computation.16.clone.1 | convolution fusion | flops 2417098752 | bytes 27935104 | tf_op jit(solution)/shard_map/while/body/eval_jaxpr/dot_general | solution.py:114
  570.2 17.6 %reduce-scatter.5.cloned.1.call-done = bf16[96,2048]{1,0:T(8,128)(2,1)} async-done(((bf16[96,4096]{1,0:T(8,128)(2,1)}), bf16[96,2048]{1,0:T(8,128)(2,1)}) %reduce-scatter.5.cloned.1.call-update) | async-done | bytes 393232 | tf_op jit(solution)/shard_map/while/body/eval_jaxpr/reduce_scatter | solution.py:141
  616.8 10.4 %fusion.85 = f32[96,3072]{1,0:T(8,128)S(1)} fusion(bf16[4096,3072]{1,0:T(8,128)(2,1)} %get-tuple-element.427, f32[96,4096]{1,0:T(8,128)S(1)} %bitcast.114, f32[4096]{0:T(1024)S(1)} %bitcast.128, f32[96]{0:T(128)S(1)} %add_rsqrt_fusion.3), kind=kOutput, calls=%fused_computation.16.clone.1 | convolution fusion | flops 2417098752 | bytes 27935104 | tf_op jit(solution)/shard_map/while/body/eval_jaxpr/dot_general | solution.py:114
  640.3 17.7 %reduce-scatter.5.cloned.1.call-done = bf16[96,2048]{1,0:T(8,128)(2,1)} async-done(((bf16[96,4096]{1,0:T(8,128)(2,1)}), bf16[96,2048]{1,0:T(8,128)(2,1)}) %reduce-scatter.5.cloned.1.call-update) | async-done | bytes 393232 | tf_op jit(solution)/shard_map/while/body/eval_jaxpr/reduce_scatter | solution.py:141
  686.9 10.4 %fusion.85 = f32[96,3072]{1,0:T(8,128)S(1)} fusion(bf16[4096,3072]{1,0:T(8,128)(2,1)} %get-tuple-element.427, f32[96,4096]{1,0:T(8,128)S(1)} %bitcast.114, f32[4096]{0:T(1024)S(1)} %bitcast.128, f32[96]{0:T(128)S(1)} %add_rsqrt_fusion.3), kind=kOutput, calls=%fused_computation.16.clone.1 | convolution fusion | flops 2417098752 | bytes 27935104 | tf_op jit(solution)/shard_map/while/body/eval_jaxpr/dot_general | solution.py:114
  710.5 17.7 %reduce-scatter.5.cloned.1.call-done = bf16[96,2048]{1,0:T(8,128)(2,1)} async-done(((bf16[96,4096]{1,0:T(8,128)(2,1)}), bf16[96,2048]{1,0:T(8,128)(2,1)}) %reduce-scatter.5.cloned.1.call-update) | async-done | bytes 393232 | tf_op jit(solution)/shard_map/while/body/eval_jaxpr/reduce_scatter | solution.py:141
  758.6 32.3 %psum.22 = bf16[32]{0:T(256)(128)(2,1)S(1)} all-reduce(bf16[32]{0:T(256)(128)(2,1)S(1)} %convert_reduce_fusion), channel_id=1, replica_groups=mesh['dp'=4,'pipe'=4,'tensor'=2] {'dp','pipe'}, use_global_device_ids=true, to_apply=%region_11.12 | all-reduce | flops 32 | bytes 128 | tf_op jit(solution)/shard_map/psum | solution.py:178
  791.6 58.0 %all-reduce.5.cloned.1.call-done = bf16[32,2048]{1,0:T(8,128)(2,1)} async-done(((bf16[32,2048]{1,0:T(8,128)(2,1)}), bf16[32,2048]{1,0:T(8,128)(2,1)}) %all-reduce.5.cloned.1.call-update) | async-done | bytes 131088 | tf_op jit(solution)/shard_map/psum | solution.py:177
  (373 shorter events, 377.2 us)
Async XLA Ops:
  7.2 173.2 %reduce-scatter.3.cloned.1.call-start = ((), (), s32[]{:S(2)}) async-start(), calls=%async_computation.4 | async-start | bytes 6684672 | tf_op jit(solution)/shard_map/reduce_scatter | solution.py:91
  182.5 13.9 %all-to-all-start = ((bf16[2,96,2048]{2,1,0:T(8,128)(2,1)}), bf16[2,96,2048]{2,1,0:T(8,128)(2,1)S(1)}, u32[]{:S(2)}, u32[]{:S(2)}) async-start(bf16[2,96,2048]{2,1,0:T(8,128)(2,1)} %pad_maximum_fusion.4), calls=%async_computation | async-start | bytes 1572864 | tf_op jit(solution)/shard_map/while/body/eval_jaxpr/all_to_all | solution.py:39
  186.0 51.2 %reduce-scatter.5.cloned.1.call-start = ((), (), s32[]{:S(2)}) async-start(), calls=%async_computation.6 | async-start | bytes 1179648 | tf_op jit(solution)/shard_map/while/body/eval_jaxpr/reduce_scatter | solution.py:141
  238.3 10.7 %collective-permute-start = (bf16[96,2048]{1,0:T(8,128)(2,1)S(1)}, bf16[96,2048]{1,0:T(8,128)(2,1)S(1)}, u32[]{:S(2)}, u32[]{:S(2)}) collective-permute-start(bf16[96,2048]{1,0:T(8,128)(2,1)S(1)} %fusion.90), channel_id=1, source_target_pairs={{6,0},{0,2},{2,4},{4,6},{7,1},{1,3},{3,5},{5,7},{14,8},{8,10},{10,... | collective-permute-start | bytes 1179656 | tf_op jit(solution)/shard_map/while/body/eval_jaxpr/ppermute | solution.py:18
  251.9 13.6 %all-to-all-start = ((bf16[2,96,2048]{2,1,0:T(8,128)(2,1)}), bf16[2,96,2048]{2,1,0:T(8,128)(2,1)S(1)}, u32[]{:S(2)}, u32[]{:S(2)}) async-start(bf16[2,96,2048]{2,1,0:T(8,128)(2,1)} %pad_maximum_fusion.4), calls=%async_computation | async-start | bytes 1572864 | tf_op jit(solution)/shard_map/while/body/eval_jaxpr/all_to_all | solution.py:39
  255.5 51.8 %reduce-scatter.5.cloned.1.call-start = ((), (), s32[]{:S(2)}) async-start(), calls=%async_computation.6 | async-start | bytes 1179648 | tf_op jit(solution)/shard_map/while/body/eval_jaxpr/reduce_scatter | solution.py:141
  308.4 10.8 %collective-permute-start = (bf16[96,2048]{1,0:T(8,128)(2,1)S(1)}, bf16[96,2048]{1,0:T(8,128)(2,1)S(1)}, u32[]{:S(2)}, u32[]{:S(2)}) collective-permute-start(bf16[96,2048]{1,0:T(8,128)(2,1)S(1)} %fusion.90), channel_id=1, source_target_pairs={{6,0},{0,2},{2,4},{4,6},{7,1},{1,3},{3,5},{5,7},{14,8},{8,10},{10,... | collective-permute-start | bytes 1179656 | tf_op jit(solution)/shard_map/while/body/eval_jaxpr/ppermute | solution.py:18
  322.1 13.6 %all-to-all-start = ((bf16[2,96,2048]{2,1,0:T(8,128)(2,1)}), bf16[2,96,2048]{2,1,0:T(8,128)(2,1)S(1)}, u32[]{:S(2)}, u32[]{:S(2)}) async-start(bf16[2,96,2048]{2,1,0:T(8,128)(2,1)} %pad_maximum_fusion.4), calls=%async_computation | async-start | bytes 1572864 | tf_op jit(solution)/shard_map/while/body/eval_jaxpr/all_to_all | solution.py:39
  325.6 51.8 %reduce-scatter.5.cloned.1.call-start = ((), (), s32[]{:S(2)}) async-start(), calls=%async_computation.6 | async-start | bytes 1179648 | tf_op jit(solution)/shard_map/while/body/eval_jaxpr/reduce_scatter | solution.py:141
  378.6 10.7 %collective-permute-start = (bf16[96,2048]{1,0:T(8,128)(2,1)S(1)}, bf16[96,2048]{1,0:T(8,128)(2,1)S(1)}, u32[]{:S(2)}, u32[]{:S(2)}) collective-permute-start(bf16[96,2048]{1,0:T(8,128)(2,1)S(1)} %fusion.90), channel_id=1, source_target_pairs={{6,0},{0,2},{2,4},{4,6},{7,1},{1,3},{3,5},{5,7},{14,8},{8,10},{10,... | collective-permute-start | bytes 1179656 | tf_op jit(solution)/shard_map/while/body/eval_jaxpr/ppermute | solution.py:18
  392.2 13.6 %all-to-all-start = ((bf16[2,96,2048]{2,1,0:T(8,128)(2,1)}), bf16[2,96,2048]{2,1,0:T(8,128)(2,1)S(1)}, u32[]{:S(2)}, u32[]{:S(2)}) async-start(bf16[2,96,2048]{2,1,0:T(8,128)(2,1)} %pad_maximum_fusion.4), calls=%async_computation | async-start | bytes 1572864 | tf_op jit(solution)/shard_map/while/body/eval_jaxpr/all_to_all | solution.py:39
  395.8 51.8 %reduce-scatter.5.cloned.1.call-start = ((), (), s32[]{:S(2)}) async-start(), calls=%async_computation.6 | async-start | bytes 1179648 | tf_op jit(solution)/shard_map/while/body/eval_jaxpr/reduce_scatter | solution.py:141
  448.7 10.7 %collective-permute-start = (bf16[96,2048]{1,0:T(8,128)(2,1)S(1)}, bf16[96,2048]{1,0:T(8,128)(2,1)S(1)}, u32[]{:S(2)}, u32[]{:S(2)}) collective-permute-start(bf16[96,2048]{1,0:T(8,128)(2,1)S(1)} %fusion.90), channel_id=1, source_target_pairs={{6,0},{0,2},{2,4},{4,6},{7,1},{1,3},{3,5},{5,7},{14,8},{8,10},{10,... | collective-permute-start | bytes 1179656 | tf_op jit(solution)/shard_map/while/body/eval_jaxpr/ppermute | solution.py:18
  462.4 13.6 %all-to-all-start = ((bf16[2,96,2048]{2,1,0:T(8,128)(2,1)}), bf16[2,96,2048]{2,1,0:T(8,128)(2,1)S(1)}, u32[]{:S(2)}, u32[]{:S(2)}) async-start(bf16[2,96,2048]{2,1,0:T(8,128)(2,1)} %pad_maximum_fusion.4), calls=%async_computation | async-start | bytes 1572864 | tf_op jit(solution)/shard_map/while/body/eval_jaxpr/all_to_all | solution.py:39
  465.9 51.9 %reduce-scatter.5.cloned.1.call-start = ((), (), s32[]{:S(2)}) async-start(), calls=%async_computation.6 | async-start | bytes 1179648 | tf_op jit(solution)/shard_map/while/body/eval_jaxpr/reduce_scatter | solution.py:141
  518.9 10.7 %collective-permute-start = (bf16[96,2048]{1,0:T(8,128)(2,1)S(1)}, bf16[96,2048]{1,0:T(8,128)(2,1)S(1)}, u32[]{:S(2)}, u32[]{:S(2)}) collective-permute-start(bf16[96,2048]{1,0:T(8,128)(2,1)S(1)} %fusion.90), channel_id=1, source_target_pairs={{6,0},{0,2},{2,4},{4,6},{7,1},{1,3},{3,5},{5,7},{14,8},{8,10},{10,... | collective-permute-start | bytes 1179656 | tf_op jit(solution)/shard_map/while/body/eval_jaxpr/ppermute | solution.py:18
  532.5 13.6 %all-to-all-start = ((bf16[2,96,2048]{2,1,0:T(8,128)(2,1)}), bf16[2,96,2048]{2,1,0:T(8,128)(2,1)S(1)}, u32[]{:S(2)}, u32[]{:S(2)}) async-start(bf16[2,96,2048]{2,1,0:T(8,128)(2,1)} %pad_maximum_fusion.4), calls=%async_computation | async-start | bytes 1572864 | tf_op jit(solution)/shard_map/while/body/eval_jaxpr/all_to_all | solution.py:39
  536.0 51.8 %reduce-scatter.5.cloned.1.call-start = ((), (), s32[]{:S(2)}) async-start(), calls=%async_computation.6 | async-start | bytes 1179648 | tf_op jit(solution)/shard_map/while/body/eval_jaxpr/reduce_scatter | solution.py:141
  602.6 13.6 %all-to-all-start = ((bf16[2,96,2048]{2,1,0:T(8,128)(2,1)}), bf16[2,96,2048]{2,1,0:T(8,128)(2,1)S(1)}, u32[]{:S(2)}, u32[]{:S(2)}) async-start(bf16[2,96,2048]{2,1,0:T(8,128)(2,1)} %pad_maximum_fusion.4), calls=%async_computation | async-start | bytes 1572864 | tf_op jit(solution)/shard_map/while/body/eval_jaxpr/all_to_all | solution.py:39
  606.2 51.9 %reduce-scatter.5.cloned.1.call-start = ((), (), s32[]{:S(2)}) async-start(), calls=%async_computation.6 | async-start | bytes 1179648 | tf_op jit(solution)/shard_map/while/body/eval_jaxpr/reduce_scatter | solution.py:141
  672.8 13.5 %all-to-all-start = ((bf16[2,96,2048]{2,1,0:T(8,128)(2,1)}), bf16[2,96,2048]{2,1,0:T(8,128)(2,1)S(1)}, u32[]{:S(2)}, u32[]{:S(2)}) async-start(bf16[2,96,2048]{2,1,0:T(8,128)(2,1)} %pad_maximum_fusion.4), calls=%async_computation | async-start | bytes 1572864 | tf_op jit(solution)/shard_map/while/body/eval_jaxpr/all_to_all | solution.py:39
  676.3 51.9 %reduce-scatter.5.cloned.1.call-start = ((), (), s32[]{:S(2)}) async-start(), calls=%async_computation.6 | async-start | bytes 1179648 | tf_op jit(solution)/shard_map/while/body/eval_jaxpr/reduce_scatter | solution.py:141
  742.9 13.5 %all-to-all-start.1 = ((bf16[2,96,2048]{2,1,0:T(8,128)(2,1)}), bf16[2,96,2048]{2,1,0:T(8,128)(2,1)S(1)}, u32[]{:S(2)}, u32[]{:S(2)}) async-start(bf16[2,96,2048]{2,1,0:T(8,128)(2,1)} %pad_maximum_fusion.2), calls=%async_computation.3 | async-start | bytes 1572864 | tf_op jit(solution)/shard_map/all_to_all | solution.py:39
  746.4 103.2 %all-reduce.5.cloned.1.call-start = ((), (), s32[]{:S(2)}) async-start(), calls=%async_computation.5 | async-start | bytes 262144 | tf_op jit(solution)/shard_map/psum | solution.py:177
  (25 other events, 363.9 us)
Sparse Core Ops, SparseCore 0:
  97.4 82.8 reduce-scatter.2
  220.6 16.5 reduce-scatter.4
  289.8 17.4 reduce-scatter.4
  359.9 17.4 reduce-scatter.4
  430.1 17.4 reduce-scatter.4
  500.2 17.5 reduce-scatter.4
  570.3 17.5 reduce-scatter.4
  640.4 17.5 reduce-scatter.4
  710.6 17.5 reduce-scatter.4
  758.6 90.9 all-reduce.4
